TPU v7x, 32 devices: a whole 2x2x4 slice. The times are simulated.
32 devices in a mesh: groups: 2 (over x), patch: 16 (over z, y, core).
Axes of the slice: x: 2, y: 2, z: 4, core: 2. Of those that a mesh axis runs over, the one named last changes fastest.
Arguments:
- queries: bfloat16 [1024, 1536], P(('groups', 'patch')), parts along dimension 0, may hold values from -8 to 8
- fresh_keys: bfloat16 [1024, 1536], P(('groups', 'patch')), parts along dimension 0, may hold values from -8 to 8
- fresh_values: bfloat16 [1024, 1536], P(('groups', 'patch')), parts along dimension 0, may hold values from -128 to 128
- stale_keys: bfloat16 [1024, 1536], P(('groups', 'patch')), parts along dimension 0, may hold values from -8 to 8
- stale_values: bfloat16 [1024, 1536], P(('groups', 'patch')), parts along dimension 0, may hold values from -128 to 128
- text_keys: bfloat16 [452, 1536], P('groups'), parts along dimension 0, may hold values from -8 to 8
- text_values: bfloat16 [452, 1536], P('groups'), parts along dimension 0, may hold values from -128 to 128
- out_weight: bfloat16 [1536, 3072], P(None, 'patch'), may hold values from -0.15625 to 0.15625
- gate_table: float32 [50, 3072], replicated, may hold values from 0.1 to 1.9
- timestep: int32 [2], P('groups'), parts along dimension 0, may hold values from 0 to 49
Outputs:
- branch: bfloat16 [1024, 3072], P(('groups', 'patch')), parts along dimension 0
There are 2 independent parts, one for each index of `groups`. A program takes and returns all parts, laid end to end along the dimension named above; an argument that names none is the same for every part. Nothing has to cross between parts.
All inputs are finite; a program needn't handle non-finite values.
Results may differ from a plain program's by a relative error of at most 0.0095.
Values may be sent and summed in bfloat16 or wider, within the bound.
A program may use at most 128 MiB of HBM per device.

v0:
```python
import functools
import math

import jax
import jax.numpy as jnp
from jax import lax
from jax.experimental import pallas as pl
from jax.experimental.pallas import tpu as pltpu
from jax.sharding import PartitionSpec as P

HEAD_DIM = 64
HEADS = 24


def from_behind(shard, axis, by):
    peers = lax.axis_size(axis)
    return lax.ppermute(shard, axis, [(i, (i + by) % peers) for i in range(peers)])


def pick_group(stacked, position):
    return lax.dynamic_index_in_dim(stacked, position, 0, keepdims=False)


def by_group(matrix, group_count):
    width = matrix.shape[1] // group_count
    return matrix.reshape(matrix.shape[0], group_count, width).transpose(1, 0, 2)


def gather_block(stacked, group_count, position):
    received = [pick_group(stacked, position)]
    for step_size in range(1, group_count):
        payload = pick_group(stacked, (position + step_size) % group_count)
        arrived = []
        for offset_by in (step_size, step_size - group_count):
            arrived.append(from_behind(payload, "patch", offset_by))
        received.append(jnp.where(position >= step_size, arrived[0], arrived[1]))
    ordered = jnp.stack(received, 0)
    order = (position - jnp.arange(group_count, dtype=jnp.int32)) % group_count
    return jnp.take(ordered, order, axis=0)


def return_block(stacked, group_count, position):
    received = [pick_group(stacked, position)]
    for step_size in range(1, group_count):
        payload = pick_group(stacked, (position + step_size) % group_count)
        arrived = []
        for offset_by in (step_size, step_size - group_count):
            arrived.append(from_behind(payload, "patch", offset_by))
        received.append(jnp.where(position >= step_size, arrived[0], arrived[1]))
    ordered = jnp.stack(received, 0)
    order = (position - jnp.arange(group_count, dtype=jnp.int32)) % group_count
    return jnp.take(ordered, order, axis=0)


def body(
    queries,
    fresh_keys,
    fresh_values,
    stale_keys,
    stale_values,
    text_keys,
    text_values,
    out_weight,
    gate_table,
    timestep,
):
    row_count = queries.shape[0]
    head_count = HEADS
    head_width = HEAD_DIM
    scaling = head_width ** (-0.5)
    group_count = math.gcd(head_count, 8)
    group_heads = head_count // group_count
    group_width = group_heads * head_width
    device_count = lax.axis_size("patch")
    position = lax.axis_index("patch") % group_count
    block_first = lax.axis_index("patch") // group_count * group_count
    local_stack = jnp.stack(
        [
            by_group(queries, group_count),
            by_group(fresh_keys, group_count),
            by_group(fresh_values, group_count),
        ],
        1,
    )
    block_stack = gather_block(local_stack, group_count, position)
    block_rows_count = group_count * row_count
    block_query = block_stack[:, 0].reshape(block_rows_count, group_heads, head_width)
    block_keys = block_stack[:, 1].reshape(block_rows_count, group_heads, head_width)
    block_values = block_stack[:, 2].reshape(block_rows_count, group_heads, head_width)
    spread_keys = jnp.tile(by_group(stale_keys, group_count), (device_count // group_count, 1, 1))
    spread_values = jnp.tile(
        by_group(stale_values, group_count), (device_count // group_count, 1, 1)
    )
    every_keys, every_values = (
        lax.all_to_all(spread_keys, "patch", split_axis=0, concat_axis=0, tiled=True),
        lax.all_to_all(spread_values, "patch", split_axis=0, concat_axis=0, tiled=True),
    )
    every_keys = every_keys.reshape(device_count * row_count, group_heads, head_width)
    every_values = every_values.reshape(device_count * row_count, group_heads, head_width)
    text_k = pick_group(by_group(text_keys, group_count), position).reshape(
        -1, group_heads, head_width
    )
    text_v = pick_group(by_group(text_values, group_count), position).reshape(
        -1, group_heads, head_width
    )
    query_patch = jnp.arange(block_rows_count, dtype=jnp.int32) // row_count
    stale_patch = jnp.arange(device_count * row_count, dtype=jnp.int32) // row_count
    stale_mask = stale_patch[None, :] != (block_first + query_patch)[:, None]
    fresh_mask = query_patch[None, :] == query_patch[:, None]

    def scored(key_block):
        return (
            jnp.einsum("qhd,khd->qhk", block_query, key_block, preferred_element_type=jnp.float32)
            * scaling
        )

    text_scores = scored(text_k)
    fresh_scores = jnp.where(fresh_mask[:, None, :], scored(block_keys), -1e30)
    stale_scores = jnp.where(stale_mask[:, None, :], scored(every_keys), -1e30)
    highest = jnp.maximum(
        jnp.maximum(jnp.max(text_scores, -1), jnp.max(fresh_scores, -1)), jnp.max(stale_scores, -1)
    )
    text_expo = jnp.exp(text_scores - highest[..., None])
    fresh_expo = jnp.exp(fresh_scores - highest[..., None])
    stale_expo = jnp.exp(stale_scores - highest[..., None])
    total = jnp.sum(text_expo, -1) + jnp.sum(fresh_expo, -1) + jnp.sum(stale_expo, -1)

    def weigh_block(expo, value_block):
        return jnp.einsum(
            "qhk,khd->qhd",
            expo.astype(jnp.bfloat16),
            value_block,
            preferred_element_type=jnp.float32,
        )

    weighted = (
        weigh_block(text_expo, text_v)
        + weigh_block(fresh_expo, block_values)
        + weigh_block(stale_expo, every_values)
    )
    block_out = (
        (weighted / total[..., None])
        .reshape(group_count, row_count, group_width)
        .astype(jnp.bfloat16)
    )
    home = return_block(block_out, group_count, position)
    attended = home.transpose(1, 0, 2).reshape(row_count, head_count * head_width)
    projected = jnp.dot(
        attended,
        lax.all_gather(out_weight, "patch", axis=1, tiled=True),
        preferred_element_type=jnp.float32,
    )
    selector = (jnp.arange(gate_table.shape[0], dtype=jnp.int32) == timestep[0]).astype(jnp.float32)
    gating = jnp.dot(selector, gate_table, precision=lax.Precision.HIGHEST)
    return (projected * gating[None, :]).astype(jnp.bfloat16)


LANES = 128
CORES = 2
HALVES = 2
PARTS = 4
NEVER = -1e30
MESH = pl.DeviceIdType.MESH


def fused_fits(mesh):
    chips = mesh.shape["patch"] // CORES
    return (
        2 * HEAD_DIM == LANES
        and mesh.shape["patch"] % (2 * CORES) == 0
        and HEADS == 3 * chips
        and chips == math.gcd(HEADS, 8)
        and chips == 4 * CORES
    )


def swap_halves(tile):
    return pltpu.roll(tile.astype(jnp.float32), HEAD_DIM, 1).astype(tile.dtype)


def low_lanes(rows):
    return lax.broadcasted_iota(jnp.int32, (rows, LANES), 1) < HEAD_DIM


def odd_pair(first, second, upper):
    low = low_lanes(first.shape[0])
    if upper:
        return jnp.where(low, swap_halves(first), second)
    return jnp.where(low, first, swap_halves(second))


def score(query, keys):
    return lax.dot_general(query, keys, (((1,), (1,)), ((), ())), preferred_element_type=jnp.float32)


def weigh(probs, values):
    return jnp.dot(probs, values, preferred_element_type=jnp.float32)


def fused_kernel(
    devices,
    q_ref,
    kf_ref,
    vf_ref,
    ks_ref,
    vs_ref,
    tk_ref,
    tv_ref,
    w_ref,
    g_ref,
    t_ref,
    out_ref,
    rows_in,
    text_in,
    gate_in,
    weights,
    weight,
    send_fresh,
    send_stale,
    fresh,
    stale,
    text,
    piece,
    pieces,
    product,
    load_sem,
    fresh_send,
    fresh_recv,
    stale_send,
    stale_recv,
    weight_send,
    weight_recv,
    piece_send,
    piece_across,
    piece_forward,
    piece_far,
    piece_recv,
    back_send,
    back_recv,
):
    groups = lax.axis_index("groups")
    me = lax.axis_index("patch")
    chips = devices // CORES
    group_count = chips
    rows = q_ref.shape[0]
    block_rows = group_count * rows
    text_rows = tk_ref.shape[0]
    part_columns = w_ref.shape[0]
    columns = CORES * part_columns
    chip, core = me // CORES, me % CORES
    block, position = me // group_count, me % group_count
    partner = me + 1 - 2 * core
    side, place = chip % 2, chip // 2
    places = chips // 2
    odd_tile = group_count + position // 2

    def device(index):
        return (groups, index)

    def remote(src, dst, send, recv, index):
        return pltpu.make_async_remote_copy(
            src_ref=src,
            dst_ref=dst,
            send_sem=send,
            recv_sem=recv,
            device_id=device(index),
            device_id_type=MESH,
        )

    def weight_rows(of_core):
        start = pl.multiple_of(of_core * part_columns, part_columns)
        return weights.at[pl.ds(start, part_columns), :]

    barrier = pltpu.get_barrier_semaphore()

    @pl.loop(1, devices)
    def _(step):
        pl.semaphore_signal(
            barrier, inc=1, device_id=device((me + step) % devices), device_id_type=MESH
        )

    loads = [
        pltpu.make_async_copy(ref, rows_in.at[i], load_sem.at[i])
        for i, ref in enumerate((q_ref, kf_ref, vf_ref, ks_ref, vs_ref))
    ]
    full_lanes = pl.ds(pl.multiple_of(position * LANES, LANES), LANES)
    odd_lanes = pl.ds(pl.multiple_of(odd_tile * LANES, LANES), LANES)
    for i, (ref, lanes) in enumerate(
        ((tk_ref, full_lanes), (tv_ref, full_lanes), (tk_ref, odd_lanes), (tv_ref, odd_lanes))
    ):
        loads.append(pltpu.make_async_copy(ref.at[:, lanes], text_in.at[i], load_sem.at[5 + i]))
    chip_columns = pl.ds(pl.multiple_of(chip * columns, LANES), columns)
    loads.append(pltpu.make_async_copy(g_ref.at[:, chip_columns], gate_in, load_sem.at[9]))
    loads.append(pltpu.make_async_copy(w_ref, weight_rows(core), load_sem.at[10]))
    for load in loads:
        load.start()

    for load in loads[:5]:
        load.wait()
    for g in range(group_count):
        own = slice(g * LANES, (g + 1) * LANES)
        tile = group_count + g // 2
        odd = slice(tile * LANES, (tile + 1) * LANES)
        upper = g % 2 == 1
        send_fresh[g, 0] = rows_in[0, :, own]
        odd_query = rows_in[0, :, odd]
        odd_query = swap_halves(odd_query) if upper else odd_query
        send_fresh[g, 1] = jnp.where(low_lanes(rows), odd_query, jnp.zeros_like(odd_query))
        send_fresh[g, 2] = rows_in[1, :, own]
        send_fresh[g, 3] = rows_in[2, :, own]
        send_fresh[g, 4] = odd_pair(rows_in[1, :, odd], rows_in[2, :, odd], upper)
        send_stale[g, 0] = rows_in[3, :, own]
        send_stale[g, 1] = rows_in[4, :, own]
        send_stale[g, 2] = odd_pair(rows_in[3, :, odd], rows_in[4, :, odd], upper)

    def patch_rows(index):
        return pl.ds(pl.multiple_of(index * rows, rows), rows)

    def fresh_copy(target, source):
        return remote(
            send_fresh.at[target],
            fresh.at[:, patch_rows(source), :],
            fresh_send.at[target],
            fresh_recv.at[source],
            block * group_count + target,
        )

    def stale_copy(target, source):
        other = (target // group_count + source // group_count) % 2
        return remote(
            send_stale.at[target % group_count],
            stale.at[other, :, patch_rows(source % group_count), :],
            stale_send.at[target],
            stale_recv.at[source],
            target,
        )

    pl.semaphore_wait(barrier, devices - 1)

    @pl.loop(1, group_count)
    def _(step):
        fresh_copy((position + step) % group_count, position).start()

    @pl.loop(1, group_count)
    def _(step):
        stale_copy(block * group_count + (position + step) % group_count, me).start()

    @pl.loop(0, group_count)
    def _(step):
        stale_copy((1 - block) * group_count + (position + step) % group_count, me).start()

    own_copies = (
        pltpu.make_async_copy(
            send_fresh.at[position],
            fresh.at[:, patch_rows(position), :],
            fresh_recv.at[position],
        ),
        pltpu.make_async_copy(
            send_stale.at[position],
            stale.at[0, :, patch_rows(position), :],
            stale_recv.at[me],
        ),
    )
    for copy in own_copies:
        copy.start()
    weight_copy = remote(w_ref, weight_rows(core), weight_send, weight_recv, partner)
    weight_copy.start()

    for load in loads[5:9]:
        load.wait()
    text[...] = jnp.zeros_like(text)
    text[0, :text_rows] = text_in[0]
    text[1, :text_rows] = text_in[1]
    text[2, :text_rows] = jnp.where(
        position % 2 == 1,
        odd_pair(text_in[2], text_in[3], True),
        odd_pair(text_in[2], text_in[3], False),
    )
    loads[9].wait()
    loads[10].wait()
    remote(w_ref, weight_rows(1 - core), weight_send, weight_recv, partner).wait_recv()
    depth = w_ref.shape[1]
    chunk = 2 * LANES

    @pl.loop(0, depth // chunk)
    def _(step):
        at = pl.ds(pl.multiple_of(step * chunk, chunk), chunk)
        weight[at, :] = weights[:, at].T

    scaling = HEAD_DIM**-0.5
    half = block_rows // HALVES
    part_rows = block_rows // PARTS
    odd_rows = part_rows // 2
    padded = text.shape[1]

    def same_patch(stacked, part, keys, first_key):
        query = lax.broadcasted_iota(jnp.int32, (stacked * half, keys), 0) % half + part * half
        key = lax.broadcasted_iota(jnp.int32, (stacked * half, keys), 1) + first_key
        return query // rows == key // rows

    def take(state, scores, values):
        highest, total, weighted = state
        peak = highest
        for each in scores:
            top = jnp.max(each, -1, keepdims=True)
            peak = top if peak is None else jnp.maximum(peak, top)
        sums = sums_of = None
        for each, value in zip(scores, values):
            expo = jnp.exp(each - peak)
            row_sum = jnp.sum(expo, -1, keepdims=True)
            product_of = weigh(expo.astype(jnp.bfloat16), value)
            sums = row_sum if sums is None else sums + row_sum
            sums_of = product_of if sums_of is None else sums_of + product_of
        if highest is None:
            return peak, sums, sums_of
        fade = jnp.exp(highest - peak)
        return peak, total * fade + sums, weighted * fade + sums_of

    @pl.loop(0, group_count)
    def _(source):
        fresh_copy(position, source).wait_recv()

    low = low_lanes(half)
    units = []
    for part in range(HALVES):
        at = slice(part * half, (part + 1) * half)
        pair_query = fresh[0, at] * jnp.asarray(scaling, fresh.dtype)
        nothing = jnp.zeros_like(pair_query)
        both = jnp.concatenate(
            [jnp.where(low, pair_query, nothing), jnp.where(low, nothing, pair_query)], 0
        )
        odd_query = fresh[1, at] * jnp.asarray(scaling, fresh.dtype)
        units.append((part, 2, 0, 1, both))
        units.append((part, 1, 2, 2, odd_query))

    states = []
    for part, stacked, kind, value_kind, query in units:
        at = slice(part * half, (part + 1) * half)
        absent = lax.broadcasted_iota(jnp.int32, (stacked * half, padded), 1) >= text_rows
        text_score = jnp.where(absent, NEVER, score(query, text[kind]))
        fresh_score = jnp.where(
            same_patch(stacked, part, half, part * half),
            score(query, fresh[kind + 2, at]),
            NEVER,
        )
        states.append(
            take(
                (None, None, None),
                (text_score, fresh_score),
                (text[value_kind], fresh[value_kind + 2, at]),
            )
        )

    @pl.loop(0, group_count)
    def _(source):
        stale_copy(me, block * group_count + source).wait_recv()

    for i, (part, stacked, kind, value_kind, query) in enumerate(units):
        own_score = jnp.where(
            same_patch(stacked, part, block_rows, 0), NEVER, score(query, stale[0, kind])
        )
        states[i] = take(states[i], (own_score,), (stale[0, value_kind],))

    @pl.loop(0, group_count)
    def _(source):
        stale_copy(me, (1 - block) * group_count + source).wait_recv()

    def column_copy(part, target_place, source):
        return remote(
            piece.at[part],
            pieces.at[part, source],
            piece_send.at[part, target_place],
            piece_recv.at[part, source],
            (target_place * 2 + side) * CORES + block,
        )

    def across_copy(part):
        return remote(
            piece.at[part],
            pieces.at[part, position],
            piece_across.at[part],
            piece_recv.at[part, position],
            (place * 2 + 1 - side) * CORES + block,
        )

    def forward_copy(part, source, index):
        return remote(
            pieces.at[part, source],
            pieces.at[part, source],
            piece_forward.at[part, index],
            piece_recv.at[part, source],
            (place * 2 + 1 - side) * CORES + core,
        )

    def far_copy(part, source, index):
        return remote(
            pieces.at[part, source],
            pieces.at[part, source],
            piece_far.at[part, index],
            piece_recv.at[part, source],
            ((1 - core) * (places - 1) * 2 + side) * CORES + core,
        )

    mate = 2 * block + 1 - place % 2
    gate = 2 - block
    at_gate = place == 2 - core
    elsewhere = place // 2 != core

    part_low = low_lanes(part_rows)
    odd_low = low_lanes(odd_rows)
    done = []
    for part in range(PARTS):
        if part % (PARTS // HALVES) == 0:
            done = []
            first_unit = 2 * (part * HALVES // PARTS)
            for i in (first_unit, first_unit + 1):
                _, _, kind, value_kind, query = units[i]
                _, total, weighted = take(
                    states[i], (score(query, stale[1, kind]),), (stale[1, value_kind],)
                )
                done.append(weighted / total)
        at = part % (PARTS // HALVES) * part_rows
        piece[part, :part_rows] = jnp.where(
            part_low, done[0][at : at + part_rows], done[0][half + at : half + at + part_rows]
        ).astype(piece.dtype)
        piece[part, part_rows:] = jnp.where(
            odd_low,
            pltpu.roll(done[1][at : at + odd_rows], HEAD_DIM, 1),
            done[1][at + odd_rows : at + part_rows],
        ).astype(piece.dtype)

        column_copy(part, gate, position).start()
        across_copy(part).start()
        column_copy(part, mate, position).start()

        @pl.when(core == block)
        def _():
            pltpu.make_async_copy(
                piece.at[part], pieces.at[part, position], piece_recv.at[part, position]
            ).start()

        @pl.when(core != block)
        def _():
            column_copy(part, place, position).start()

    def column_source(index, of_side):
        return index // CORES * 2 * CORES + of_side * CORES + index % CORES

    column_pieces = group_count // 2

    for part in range(PARTS):

        @pl.loop(0, column_pieces)
        def _(index):
            index = (index + (1 - core) * CORES) % column_pieces
            source = column_source(index, side)
            column_copy(part, place, source).wait_recv()

            @pl.when(at_gate)
            def _():
                far_copy(part, source, index).start()

            @pl.when(elsewhere | (index // CORES != place % 2))
            def _():
                forward_copy(part, source, index).start()

    def back_copy(target, source):
        return remote(
            product.at[target],
            out_ref.at[:, pl.ds(pl.multiple_of(source * columns, LANES), columns)],
            back_send.at[target],
            back_recv.at[source],
            core * group_count + target,
        )

    gating = gate_in[pl.ds(t_ref[0], 1), :]
    patches = group_count // PARTS
    for part in range(PARTS):

        @pl.loop(0, column_pieces)
        def _(index):
            column_copy(part, place, column_source(index, 1 - side)).wait_recv()

        tiles = [pieces[part, g, :part_rows] for g in range(group_count)]
        for pair in range(group_count // 2):
            even = pieces[part, 2 * pair, part_rows:]
            upper = pieces[part, 2 * pair + 1, part_rows:]
            top = jnp.where(odd_low, even, swap_halves(upper))
            bottom = jnp.where(odd_low, swap_halves(even), upper)
            tiles.append(jnp.concatenate([top, bottom], 0))
        attended = jnp.concatenate(tiles, 1)
        projected = jnp.dot(attended, weight[...], preferred_element_type=jnp.float32)
        product[part * patches : (part + 1) * patches] = (
            (projected * gating).astype(product.dtype).reshape(patches, rows, columns)
        )

        @pl.loop(0, patches)
        def _(step):
            target = part * patches + (position + step) % patches

            @pl.when(core * group_count + target != me)
            def _():
                back_copy(target, chip).start()

        @pl.when((core == block) & (position // patches == part))
        def _():
            pltpu.make_async_copy(
                product.at[position],
                out_ref.at[:, chip_columns],
                back_recv.at[chip],
            ).start()

    @pl.loop(1, group_count)
    def _(step):
        fresh_copy((position + step) % group_count, position).wait_send()

    @pl.loop(1, devices)
    def _(step):
        stale_copy((me + step) % devices, me).wait_send()

    weight_copy.wait_send()

    for part in range(PARTS):

        column_copy(part, gate, position).wait_send()
        across_copy(part).wait_send()
        column_copy(part, mate, position).wait_send()

        @pl.when(core != block)
        def _():
            column_copy(part, place, position).wait_send()

        @pl.loop(0, column_pieces)
        def _(index):
            source = column_source(index, side)

            @pl.when(at_gate)
            def _():
                far_copy(part, source, index).wait_send()

            @pl.when(elsewhere | (index // CORES != place % 2))
            def _():
                forward_copy(part, source, index).wait_send()

    @pl.loop(0, group_count)
    def _(target):
        @pl.when(core * group_count + target != me)
        def _():
            back_copy(target, chip).wait_send()

    @pl.loop(0, chips)
    def _(source):
        back_copy(position, source).wait_recv()


def fused_body(
    queries,
    fresh_keys,
    fresh_values,
    stale_keys,
    stale_values,
    text_keys,
    text_values,
    out_weight,
    gate_table,
    timestep,
):
    devices = lax.axis_size("patch")
    chips = devices // CORES
    group_count = chips
    rows, width = queries.shape
    block_rows = group_count * rows
    piece_rows = (block_rows + block_rows // 2) // PARTS
    text_rows = text_keys.shape[0]
    padded = -(-text_rows // LANES) * LANES
    depth, part_columns = out_weight.shape
    columns = CORES * part_columns
    bf16 = jnp.bfloat16
    dma = pltpu.SemaphoreType.DMA
    anywhere = pl.BlockSpec(memory_space=pl.ANY)
    return pl.pallas_call(
        functools.partial(fused_kernel, devices),
        out_shape=jax.ShapeDtypeStruct((rows, part_columns * devices), bf16),
        in_specs=[anywhere] * 9 + [pl.BlockSpec(memory_space=pltpu.SMEM)],
        out_specs=anywhere,
        scratch_shapes=[
            pltpu.VMEM((5, rows, width), bf16),
            pltpu.VMEM((4, text_rows, LANES), bf16),
            pltpu.VMEM((gate_table.shape[0], columns), jnp.float32),
            pltpu.VMEM((columns, depth), bf16),
            pltpu.VMEM((depth, columns), bf16),
            pltpu.VMEM((group_count, 5, rows, LANES), bf16),
            pltpu.VMEM((group_count, 3, rows, LANES), bf16),
            pltpu.VMEM((5, block_rows, LANES), bf16),
            pltpu.VMEM((2, 3, block_rows, LANES), bf16),
            pltpu.VMEM((3, padded, LANES), bf16),
            pltpu.VMEM((PARTS, piece_rows, LANES), bf16),
            pltpu.VMEM((PARTS, group_count, piece_rows, LANES), bf16),
            pltpu.VMEM((group_count, rows, columns), bf16),
            dma((11,)),
            dma((group_count,)),
            dma((group_count,)),
            dma((devices,)),
            dma((devices,)),
            dma,
            dma,
            dma((PARTS, chips // 2)),
            dma((PARTS,)),
            dma((PARTS, group_count // 2)),
            dma((PARTS, group_count // 2)),
            dma((PARTS, group_count)),
            dma((group_count,)),
            dma((chips,)),
        ],
        compiler_params=pltpu.CompilerParams(collective_id=0, has_side_effects=True),
    )(
        queries,
        fresh_keys,
        fresh_values,
        stale_keys,
        stale_values,
        text_keys,
        text_values,
        out_weight.T,
        gate_table,
        timestep,
    )


def solution(mesh):
    in_specs = (
        P(("groups", "patch"), None),
        P(("groups", "patch"), None),
        P(("groups", "patch"), None),
        P(("groups", "patch"), None),
        P(("groups", "patch"), None),
        P("groups", None),
        P("groups", None),
        P(None, "patch"),
        P(),
        P("groups"),
    )
    out_specs = P(("groups", "patch"), None)
    chosen = fused_body if fused_fits(mesh) else body
    return jax.shard_map(chosen, mesh=mesh, in_specs=in_specs, out_specs=out_specs, check_vma=False)
```

profile of v0, /device:TPU:1, one launch (start us, length us, event | category | flops | bytes accessed | tf_op | source)
XLA Modules:
  0.0 37.2 jit_solution(15205006484569292070)
XLA Ops:
  0.7 35.0 %shard_map.100 = bf16[32,3072]{1,0:T(8,128)(2,1)} custom-call(bf16[32,1536]{1,0:T(8,128)(2,1)} %q_ref.1, bf16[32,1536]{1,0:T(8,128)(2,1)} %kf_ref.1, bf16[32,1536]{1,0:T(8,128)(2,1)} %vf_ref.1, bf16[32,1536]{1,0:T(8,128)(2,1)} %ks_ref.1, bf16[32,1536]{1,0:T(8,128)(2,1)} %vs_ref.1, bf16[226,1536]{1,0:T(8,128)(2,1)} %tk_ref.1, bf16[226,1536]{1,0:T(8,128)(2,1)} %tv_ref.1, ...), custom_call_target="tpu_custom_call" | custom-call | tf_op jit(solution)/shard_map/pallas_call | solution.py:681
  35.6 1.6 %copy.13 = bf16[32,3072]{1,0:T(8,128)(2,1)} copy(bf16[32,3072]{1,0:T(8,128)(2,1)} %shard_map.100) | data formatting | bytes 393216
where the time goes:
time: 37.8 us; the launch traced here: 37.2 us
  Pallas kernels  35 us (93%)
  local copies, waits for them, and re-layouts  1.62 us (4%)
  between operations  0.66 us (2%)
    pallas_call x1, Pallas kernels, fused_body(): pl.pallas_call(functools.partial(fused_kernel, devices), out_shape=jax.Sh...  35 us
    unnamed x1, local copies, waits for them, and re-layouts  1.62 us

commit v1 on v0

--- a/solution.py
+++ b/solution.py
@@ -680,9 +680,9 @@
     anywhere = pl.BlockSpec(memory_space=pl.ANY)
     return pl.pallas_call(
         functools.partial(fused_kernel, devices),
-        out_shape=jax.ShapeDtypeStruct((rows, part_columns * devices), bf16),
+        out_shape=pltpu.VMEM((rows, part_columns * devices), bf16),
         in_specs=[anywhere] * 9 + [pl.BlockSpec(memory_space=pltpu.SMEM)],
-        out_specs=anywhere,
+        out_specs=pl.BlockSpec(memory_space=pltpu.VMEM),
         scratch_shapes=[
             pltpu.VMEM((5, rows, width), bf16),
             pltpu.VMEM((4, text_rows, LANES), bf16),

time: 37.8 us -> 36.8 us (0.974)
  local copies, waits for them, and re-layouts: 1.62 us -> 0.68 us
    unnamed x1, local copies, waits for them, and re-layouts: 1.62 us -> 0.68 us
where the time goes in v1:
time: 36.8 us; the launch traced here: 36.2 us
  Pallas kernels  34.9 us (95%)
  local copies, waits for them, and re-layouts  0.68 us (2%)
  between operations  0.66 us (2%)
    pallas_call x1, Pallas kernels, fused_body(): pl.pallas_call(functools.partial(fused_kernel, devices), out_shape=pltpu....  34.9 us

profile of v1, /device:TPU:1, one launch (start us, length us, event | category | flops | bytes accessed | tf_op | source)
XLA Modules:
  0.0 36.2 jit_solution(5709711071700906841)
XLA Ops:
  0.7 34.9 %shard_map.100 = bf16[32,3072]{1,0:T(8,128)(2,1)S(1)} custom-call(bf16[32,1536]{1,0:T(8,128)(2,1)} %q_ref.1, bf16[32,1536]{1,0:T(8,128)(2,1)} %kf_ref.1, bf16[32,1536]{1,0:T(8,128)(2,1)} %vf_ref.1, bf16[32,1536]{1,0:T(8,128)(2,1)} %ks_ref.1, bf16[32,1536]{1,0:T(8,128)(2,1)} %vs_ref.1, bf16[226,1536]{1,0:T(8,128)(2,1)} %tk_ref.1, bf16[226,1536]{1,0:T(8,128)(2,1)} %tv_ref.1, ...), custom_call_target="tpu_custom_call" | custom-call | tf_op jit(solution)/shard_map/pallas_call | solution.py:681
  35.5 0.7 %copy.12 = bf16[32,3072]{1,0:T(8,128)(2,1)} copy(bf16[32,3072]{1,0:T(8,128)(2,1)S(1)} %shard_map.100) | data formatting | bytes 393216

commit v2 on v1

--- a/solution.py
+++ b/solution.py
@@ -157,7 +157,8 @@
 
 LANES = 128
 CORES = 2
-HALVES = 2
+LINES = 4
+HALVES = 1
 PARTS = 4
 NEVER = -1e30
 MESH = pl.DeviceIdType.MESH
@@ -215,19 +216,19 @@
     gate_in,
     weights,
     weight,
-    send_fresh,
-    send_stale,
-    fresh,
-    stale,
+    send,
+    near,
+    away,
     text,
     piece,
     pieces,
     product,
     load_sem,
-    fresh_send,
-    fresh_recv,
-    stale_send,
-    stale_recv,
+    seen,
+    near_send,
+    near_recv,
+    away_send,
+    away_recv,
     weight_send,
     weight_recv,
     piece_send,
@@ -271,18 +272,30 @@
         start = pl.multiple_of(of_core * part_columns, part_columns)
         return weights.at[pl.ds(start, part_columns), :]
 
-    barrier = pltpu.get_barrier_semaphore()
-
-    @pl.loop(1, devices)
-    def _(step):
-        pl.semaphore_signal(
-            barrier, inc=1, device_id=device((me + step) % devices), device_id_type=MESH
-        )
-
     loads = [
         pltpu.make_async_copy(ref, rows_in.at[i], load_sem.at[i])
         for i, ref in enumerate((q_ref, kf_ref, vf_ref, ks_ref, vs_ref))
     ]
+    for load in loads:
+        load.start()
+
+    barrier = pltpu.get_barrier_semaphore()
+    has_below, has_above = place > 0, place < places - 1
+
+    def greet(index):
+        pl.semaphore_signal(barrier, inc=1, device_id=device(index), device_id_type=MESH)
+
+    @pl.when(has_above)
+    def _():
+        greet(me + LINES)
+
+    @pl.when(has_below)
+    def _():
+        greet(me - LINES)
+
+    for step in range(1, LINES):
+        greet(place * LINES + (me + step) % LINES)
+
     full_lanes = pl.ds(pl.multiple_of(position * LANES, LANES), LANES)
     odd_lanes = pl.ds(pl.multiple_of(odd_tile * LANES, LANES), LANES)
     for i, (ref, lanes) in enumerate(
@@ -292,8 +305,46 @@
     chip_columns = pl.ds(pl.multiple_of(chip * columns, LANES), columns)
     loads.append(pltpu.make_async_copy(g_ref.at[:, chip_columns], gate_in, load_sem.at[9]))
     loads.append(pltpu.make_async_copy(w_ref, weight_rows(core), load_sem.at[10]))
-    for load in loads:
+    for load in loads[5:]:
         load.start()
+
+    pl.semaphore_wait(
+        barrier, LINES - 1 + has_below.astype(jnp.int32) + has_above.astype(jnp.int32)
+    )
+
+    def tell(index, about):
+        pl.semaphore_signal(seen.at[about], inc=1, device_id=device(index), device_id_type=MESH)
+
+    @pl.when(has_above)
+    def _():
+        tell(me + LINES, place)
+
+    @pl.when(has_below)
+    def _():
+        tell(me - LINES, place)
+
+    def hear(other):
+        pl.semaphore_wait(seen.at[other], 1)
+
+        @pl.when((other < place) & has_above)
+        def _():
+            tell(me + LINES, other)
+
+        @pl.when((other > place) & has_below)
+        def _():
+            tell(me - LINES, other)
+
+    @pl.when(has_below & has_above)
+    def _():
+        @pl.loop(0, place)
+        def _(step):
+            hear(place - 1 - step)
+
+        @pl.when(block == 1)
+        def _():
+            @pl.loop(place + 1, places)
+            def _(other):
+                hear(other)
 
     for load in loads[:5]:
         load.wait()
@@ -302,67 +353,92 @@
         tile = group_count + g // 2
         odd = slice(tile * LANES, (tile + 1) * LANES)
         upper = g % 2 == 1
-        send_fresh[g, 0] = rows_in[0, :, own]
-        odd_query = rows_in[0, :, odd]
-        odd_query = swap_halves(odd_query) if upper else odd_query
-        send_fresh[g, 1] = jnp.where(low_lanes(rows), odd_query, jnp.zeros_like(odd_query))
-        send_fresh[g, 2] = rows_in[1, :, own]
-        send_fresh[g, 3] = rows_in[2, :, own]
-        send_fresh[g, 4] = odd_pair(rows_in[1, :, odd], rows_in[2, :, odd], upper)
-        send_stale[g, 0] = rows_in[3, :, own]
-        send_stale[g, 1] = rows_in[4, :, own]
-        send_stale[g, 2] = odd_pair(rows_in[3, :, odd], rows_in[4, :, odd], upper)
-
-    def patch_rows(index):
-        return pl.ds(pl.multiple_of(index * rows, rows), rows)
-
-    def fresh_copy(target, source):
+        half_rows = rows // 2
+        sent = (
+            rows_in[3, :, own],
+            rows_in[4, :, own],
+            odd_pair(rows_in[3, :, odd], rows_in[4, :, odd], upper),
+            rows_in[0, :, own],
+            rows_in[1, :, own],
+            rows_in[2, :, own],
+            odd_pair(rows_in[1, :, odd], rows_in[2, :, odd], upper),
+            odd_pair(rows_in[0, :half_rows, odd], rows_in[0, half_rows:, odd], upper),
+        )
+        for i, tile_rows in enumerate(sent):
+            send[g, i * rows : i * rows + tile_rows.shape[0]] = tile_rows
+
+    def near_copy(target, source):
         return remote(
-            send_fresh.at[target],
-            fresh.at[:, patch_rows(source), :],
-            fresh_send.at[target],
-            fresh_recv.at[source],
+            send.at[target],
+            near.at[source],
+            near_send.at[target],
+            near_recv.at[source],
             block * group_count + target,
         )
 
-    def stale_copy(target, source):
-        other = (target // group_count + source // group_count) % 2
+    def away_copy(target, source):
         return remote(
-            send_stale.at[target % group_count],
-            stale.at[other, :, patch_rows(source % group_count), :],
-            stale_send.at[target],
-            stale_recv.at[source],
-            target,
-        )
-
-    pl.semaphore_wait(barrier, devices - 1)
-
-    @pl.loop(1, group_count)
-    def _(step):
-        fresh_copy((position + step) % group_count, position).start()
-
-    @pl.loop(1, group_count)
-    def _(step):
-        stale_copy(block * group_count + (position + step) % group_count, me).start()
-
-    @pl.loop(0, group_count)
-    def _(step):
-        stale_copy((1 - block) * group_count + (position + step) % group_count, me).start()
-
-    own_copies = (
-        pltpu.make_async_copy(
-            send_fresh.at[position],
-            fresh.at[:, patch_rows(position), :],
-            fresh_recv.at[position],
-        ),
-        pltpu.make_async_copy(
-            send_stale.at[position],
-            stale.at[0, :, patch_rows(position), :],
-            stale_recv.at[me],
-        ),
-    )
-    for copy in own_copies:
-        copy.start()
+            send.at[target, pl.ds(0, 3 * rows)],
+            away.at[source],
+            away_send.at[target],
+            away_recv.at[source],
+            (1 - block) * group_count + target,
+        )
+
+    def send_plane(other):
+        @pl.loop(0, LINES)
+        def _(step):
+            target = other % 2 * LINES + (me + step) % LINES
+
+            @pl.when(other // 2 == block)
+            def _():
+                near_copy(target, position).start()
+
+            @pl.when(other // 2 != block)
+            def _():
+                away_copy(target, position).start()
+
+    def send_here():
+        @pl.loop(1, LINES)
+        def _(step):
+            near_copy(place % 2 * LINES + (me + step) % LINES, position).start()
+
+    @pl.when(block == 0)
+    def _():
+        send_here()
+
+        @pl.when(has_below)
+        def _():
+            send_plane(place - 1)
+
+        @pl.loop(place + 1, places)
+        def _(other):
+            hear(other)
+            send_plane(other)
+
+    @pl.when(block == 1)
+    def _():
+        @pl.when(jnp.logical_not(has_above))
+        def _():
+            @pl.loop(0, place)
+            def _(step):
+                hear(place - 1 - step)
+
+        @pl.when(has_above)
+        def _():
+            send_plane(2 * block + 1 - place % 2)
+            send_plane(1)
+            send_plane(0)
+            send_here()
+
+        @pl.when(jnp.logical_not(has_above))
+        def _():
+            send_plane(0)
+            send_plane(1)
+            send_plane(2 * block + 1 - place % 2)
+            send_here()
+
+    pltpu.make_async_copy(send.at[position], near.at[position], near_recv.at[position]).start()
     weight_copy = remote(w_ref, weight_rows(core), weight_send, weight_recv, partner)
     weight_copy.start()
 
@@ -393,77 +469,77 @@
     odd_rows = part_rows // 2
     padded = text.shape[1]
 
-    def same_patch(stacked, part, keys, first_key):
-        query = lax.broadcasted_iota(jnp.int32, (stacked * half, keys), 0) % half + part * half
-        key = lax.broadcasted_iota(jnp.int32, (stacked * half, keys), 1) + first_key
-        return query // rows == key // rows
-
-    def take(state, scores, values):
-        highest, total, weighted = state
-        peak = highest
-        for each in scores:
-            top = jnp.max(each, -1, keepdims=True)
-            peak = top if peak is None else jnp.maximum(peak, top)
-        sums = sums_of = None
-        for each, value in zip(scores, values):
-            expo = jnp.exp(each - peak)
-            row_sum = jnp.sum(expo, -1, keepdims=True)
-            product_of = weigh(expo.astype(jnp.bfloat16), value)
-            sums = row_sum if sums is None else sums + row_sum
-            sums_of = product_of if sums_of is None else sums_of + product_of
-        if highest is None:
-            return peak, sums, sums_of
+    def same_patch(stacked):
+        query = lax.broadcasted_iota(jnp.int32, (stacked * half, 1), 0) % half // rows
+        key = lax.broadcasted_iota(jnp.int32, (1, half), 1) // rows
+        return query == key
+
+    def lane_sums(expo):
+        sums = expo[:, :LANES]
+        for first in range(LANES, expo.shape[1], LANES):
+            sums = sums + expo[:, first : first + LANES]
+        return sums
+
+    def finish(state, scores, values):
+        highest, sums, weighted = state
+        peak = jnp.maximum(highest, jnp.max(scores, -1, keepdims=True))
         fade = jnp.exp(highest - peak)
-        return peak, total * fade + sums, weighted * fade + sums_of
+        expo = jnp.exp(scores - peak)
+        total = jnp.sum(sums * fade + lane_sums(expo), -1, keepdims=True)
+        weighted = weighted * fade + weigh(expo.astype(jnp.bfloat16), values)
+        return weighted / total
 
     @pl.loop(0, group_count)
     def _(source):
-        fresh_copy(position, source).wait_recv()
+        near_copy(position, source).wait_recv()
+
+    def tiles_of(ref, index, first=0, last=group_count):
+        at = slice(index * rows, (index + 1) * rows)
+        return jnp.concatenate([ref[source, at] for source in range(first, last)], 0)
 
     low = low_lanes(half)
+    half_low = low_lanes(rows // 2)
+    per_half = group_count // HALVES
     units = []
     for part in range(HALVES):
-        at = slice(part * half, (part + 1) * half)
-        pair_query = fresh[0, at] * jnp.asarray(scaling, fresh.dtype)
+        mine = (part * per_half, (part + 1) * per_half)
+        pair_query = tiles_of(near, 3, *mine) * jnp.asarray(scaling, near.dtype)
         nothing = jnp.zeros_like(pair_query)
         both = jnp.concatenate(
             [jnp.where(low, pair_query, nothing), jnp.where(low, nothing, pair_query)], 0
         )
-        odd_query = fresh[1, at] * jnp.asarray(scaling, fresh.dtype)
-        units.append((part, 2, 0, 1, both))
-        units.append((part, 1, 2, 2, odd_query))
+        odd_query = []
+        for source in range(*mine):
+            packed = near[source, 7 * rows :]
+            for each in (packed, swap_halves(packed)):
+                odd_query.append(jnp.where(half_low, each, jnp.zeros_like(each)))
+        odd_query = jnp.concatenate(odd_query, 0) * jnp.asarray(scaling, near.dtype)
+        units.append((part, 2, (4, 5, 0, 1), text[0], text[1], both))
+        units.append((part, 1, (6, 6, 2, 2), text[2], text[2], odd_query))
 
     states = []
-    for part, stacked, kind, value_kind, query in units:
-        at = slice(part * half, (part + 1) * half)
-        absent = lax.broadcasted_iota(jnp.int32, (stacked * half, padded), 1) >= text_rows
-        text_score = jnp.where(absent, NEVER, score(query, text[kind]))
-        fresh_score = jnp.where(
-            same_patch(stacked, part, half, part * half),
-            score(query, fresh[kind + 2, at]),
-            NEVER,
-        )
-        states.append(
-            take(
-                (None, None, None),
-                (text_score, fresh_score),
-                (text[value_kind], fresh[value_kind + 2, at]),
-            )
-        )
+    last = padded - LANES
+    absent = lax.broadcasted_iota(jnp.int32, (1, LANES), 1) >= text_rows - last
+    for part, stacked, kinds, text_key, text_value, query in units:
+        mine = (part * per_half, (part + 1) * per_half)
+        new_key, new_value, old_key, old_value = (tiles_of(near, kind, *mine) for kind in kinds)
+        scores = score(query, jnp.concatenate([text_key, old_key, new_key], 0))
+        same = same_patch(stacked)
+        mixed = jnp.where(same, scores[:, padded + half :], scores[:, padded : padded + half])
+        scores = jnp.concatenate(
+            [scores[:, :last], jnp.where(absent, NEVER, scores[:, last:padded]), mixed], 1
+        )
+        peak = jnp.max(scores, -1, keepdims=True)
+        expo = jnp.exp(scores - peak)
+        mixed = expo[:, padded:]
+        probs = [expo[:, :padded], jnp.where(same, 0.0, mixed), jnp.where(same, mixed, 0.0)]
+        probs = jnp.concatenate([each.astype(jnp.bfloat16) for each in probs], 1)
+        values = jnp.concatenate([text_value, old_value, new_value], 0)
+        states.append((peak, lane_sums(expo), weigh(probs, values)))
 
     @pl.loop(0, group_count)
     def _(source):
-        stale_copy(me, block * group_count + source).wait_recv()
-
-    for i, (part, stacked, kind, value_kind, query) in enumerate(units):
-        own_score = jnp.where(
-            same_patch(stacked, part, block_rows, 0), NEVER, score(query, stale[0, kind])
-        )
-        states[i] = take(states[i], (own_score,), (stale[0, value_kind],))
-
-    @pl.loop(0, group_count)
-    def _(source):
-        stale_copy(me, (1 - block) * group_count + source).wait_recv()
+        away_copy(position, source).wait_recv()
 
     def column_copy(part, target_place, source):
         return remote(
@@ -514,11 +590,9 @@
             done = []
             first_unit = 2 * (part * HALVES // PARTS)
             for i in (first_unit, first_unit + 1):
-                _, _, kind, value_kind, query = units[i]
-                _, total, weighted = take(
-                    states[i], (score(query, stale[1, kind]),), (stale[1, value_kind],)
-                )
-                done.append(weighted / total)
+                _, _, kinds, _, _, query = units[i]
+                key, value = (tiles_of(away, kind) for kind in kinds[2:])
+                done.append(finish(states[i], score(query, key), value))
         at = part % (PARTS // HALVES) * part_rows
         piece[part, :part_rows] = jnp.where(
             part_low, done[0][at : at + part_rows], done[0][half + at : half + at + part_rows]
@@ -612,11 +686,11 @@
 
     @pl.loop(1, group_count)
     def _(step):
-        fresh_copy((position + step) % group_count, position).wait_send()
-
-    @pl.loop(1, devices)
-    def _(step):
-        stale_copy((me + step) % devices, me).wait_send()
+        near_copy((position + step) % group_count, position).wait_send()
+
+    @pl.loop(0, group_count)
+    def _(target):
+        away_copy(target, position).wait_send()
 
     weight_copy.wait_send()
 
@@ -689,19 +763,19 @@
             pltpu.VMEM((gate_table.shape[0], columns), jnp.float32),
             pltpu.VMEM((columns, depth), bf16),
             pltpu.VMEM((depth, columns), bf16),
-            pltpu.VMEM((group_count, 5, rows, LANES), bf16),
-            pltpu.VMEM((group_count, 3, rows, LANES), bf16),
-            pltpu.VMEM((5, block_rows, LANES), bf16),
-            pltpu.VMEM((2, 3, block_rows, LANES), bf16),
+            pltpu.VMEM((group_count, 7 * rows + rows // 2, LANES), bf16),
+            pltpu.VMEM((group_count, 7 * rows + rows // 2, LANES), bf16),
+            pltpu.VMEM((group_count, 3 * rows, LANES), bf16),
             pltpu.VMEM((3, padded, LANES), bf16),
             pltpu.VMEM((PARTS, piece_rows, LANES), bf16),
             pltpu.VMEM((PARTS, group_count, piece_rows, LANES), bf16),
             pltpu.VMEM((group_count, rows, columns), bf16),
             dma((11,)),
+            pltpu.SemaphoreType.REGULAR((chips // 2,)),
             dma((group_count,)),
             dma((group_count,)),
-            dma((devices,)),
-            dma((devices,)),
+            dma((group_count,)),
+            dma((group_count,)),
             dma,
             dma,
             dma((PARTS, chips // 2)),

time: 36.8 us -> 36 us (0.978); the launches traced: 36.2 us -> 35.9 us
  Pallas kernels: 34.9 us -> 34.5 us
where the time goes in v2:
time: 36 us; the launch traced here: 35.9 us
  Pallas kernels  34.5 us (96%)
  local copies, waits for them, and re-layouts  0.68 us (2%)
  between operations  0.66 us (2%)
    pallas_call x1, Pallas kernels, fused_body(): pl.pallas_call(functools.partial(fused_kernel, devices), out_shape=pltpu....  34.5 us

profile of v2, /device:TPU:1, one launch (start us, length us, event | category | flops | bytes accessed | tf_op | source)
XLA Modules:
  0.0 35.9 jit_solution(5544452002856782397)
XLA Ops:
  0.7 34.5 %shard_map.100 = bf16[32,3072]{1,0:T(8,128)(2,1)S(1)} custom-call(bf16[32,1536]{1,0:T(8,128)(2,1)} %q_ref.1, bf16[32,1536]{1,0:T(8,128)(2,1)} %kf_ref.1, bf16[32,1536]{1,0:T(8,128)(2,1)} %vf_ref.1, bf16[32,1536]{1,0:T(8,128)(2,1)} %ks_ref.1, bf16[32,1536]{1,0:T(8,128)(2,1)} %vs_ref.1, bf16[226,1536]{1,0:T(8,128)(2,1)} %tk_ref.1, bf16[226,1536]{1,0:T(8,128)(2,1)} %tv_ref.1, ...), custom_call_target="tpu_custom_call" | custom-call | tf_op jit(solution)/shard_map/pallas_call | solution.py:755
  35.2 0.7 %copy.12 = bf16[32,3072]{1,0:T(8,128)(2,1)} copy(bf16[32,3072]{1,0:T(8,128)(2,1)S(1)} %shard_map.100) | data formatting | bytes 393216

commit v3 on v2

--- a/solution.py
+++ b/solution.py
@@ -604,8 +604,10 @@
         ).astype(piece.dtype)
 
         column_copy(part, gate, position).start()
+        column_copy(part, mate, position).start()
         across_copy(part).start()
-        column_copy(part, mate, position).start()
+
+    for part in range(PARTS):
 
         @pl.when(core == block)
         def _():

time: 36 us -> 36 us (level)
  no operation moved by 1% of the time
where the time goes in v3:
time: 36 us; the launch traced here: 35.9 us
  Pallas kernels  34.5 us (96%)
  local copies, waits for them, and re-layouts  0.68 us (2%)
  between operations  0.66 us (2%)
    pallas_call x1, Pallas kernels, fused_body(): pl.pallas_call(functools.partial(fused_kernel, devices), out_shape=pltpu....  34.5 us

profile of v3, /device:TPU:1, one launch (start us, length us, event | category | flops | bytes accessed | tf_op | source)
XLA Modules:
  0.0 35.9 jit_solution(16871562157423612578)
XLA Ops:
  0.7 34.5 %shard_map.100 = bf16[32,3072]{1,0:T(8,128)(2,1)S(1)} custom-call(bf16[32,1536]{1,0:T(8,128)(2,1)} %q_ref.1, bf16[32,1536]{1,0:T(8,128)(2,1)} %kf_ref.1, bf16[32,1536]{1,0:T(8,128)(2,1)} %vf_ref.1, bf16[32,1536]{1,0:T(8,128)(2,1)} %ks_ref.1, bf16[32,1536]{1,0:T(8,128)(2,1)} %vs_ref.1, bf16[226,1536]{1,0:T(8,128)(2,1)} %tk_ref.1, bf16[226,1536]{1,0:T(8,128)(2,1)} %tv_ref.1, ...), custom_call_target="tpu_custom_call" | custom-call | tf_op jit(solution)/shard_map/pallas_call | solution.py:757
  35.2 0.7 %copy.12 = bf16[32,3072]{1,0:T(8,128)(2,1)} copy(bf16[32,3072]{1,0:T(8,128)(2,1)S(1)} %shard_map.100) | data formatting | bytes 393216

commit v4 on v3

--- a/solution.py
+++ b/solution.py
@@ -405,16 +405,19 @@
 
     @pl.when(block == 0)
     def _():
-        send_here()
-
         @pl.when(has_below)
         def _():
             send_plane(place - 1)
+            send_here()
 
         @pl.loop(place + 1, places)
         def _(other):
             hear(other)
             send_plane(other)
+
+            @pl.when(jnp.logical_not(has_below) & (other == place + 1))
+            def _():
+                send_here()
 
     @pl.when(block == 1)
     def _():

time: 36 us -> 36 us (level)
  no operation moved by 1% of the time
where the time goes in v4:
time: 36 us; the launch traced here: 35.9 us
  Pallas kernels  34.5 us (96%)
  local copies, waits for them, and re-layouts  0.68 us (2%)
  between operations  0.66 us (2%)
    pallas_call x1, Pallas kernels, fused_body(): pl.pallas_call(functools.partial(fused_kernel, devices), out_shape=pltpu....  34.5 us

profile of v4, /device:TPU:1, one launch (start us, length us, event | category | flops | bytes accessed | tf_op | source)
XLA Modules:
  0.0 35.9 jit_solution(13774884163180225966)
XLA Ops:
  0.7 34.5 %shard_map.100 = bf16[32,3072]{1,0:T(8,128)(2,1)S(1)} custom-call(bf16[32,1536]{1,0:T(8,128)(2,1)} %q_ref.1, bf16[32,1536]{1,0:T(8,128)(2,1)} %kf_ref.1, bf16[32,1536]{1,0:T(8,128)(2,1)} %vf_ref.1, bf16[32,1536]{1,0:T(8,128)(2,1)} %ks_ref.1, bf16[32,1536]{1,0:T(8,128)(2,1)} %vs_ref.1, bf16[226,1536]{1,0:T(8,128)(2,1)} %tk_ref.1, bf16[226,1536]{1,0:T(8,128)(2,1)} %tv_ref.1, ...), custom_call_target="tpu_custom_call" | custom-call | tf_op jit(solution)/shard_map/pallas_call | solution.py:760
  35.2 0.7 %copy.12 = bf16[32,3072]{1,0:T(8,128)(2,1)} copy(bf16[32,3072]{1,0:T(8,128)(2,1)S(1)} %shard_map.100) | data formatting | bytes 393216
